TPU v7x, 32 devices: a whole 2x2x4 slice. The times are simulated.
32 devices in a mesh: unit: 4 (over z), bank: 4 (over x, core), zero: 2 (over y).
Axes of the slice: x: 2, y: 2, z: 4, core: 2. Of those that a mesh axis runs over, the one named last changes fastest.
Arguments:
- train_down: float32 [256, 1024, 2048], P(('unit', 'bank'), None, 'zero'), parts along dimension 0, may hold values from -0.25 to 0.25
- router_weight: float32 [8192, 64], P(('unit', 'zero'), 'bank'), parts along dimension 0, may hold values from -0.125 to 0.125
- router_gain: float32 [8192], P(('unit', 'zero')), parts along dimension 0, may hold values from 0.25 to 1.75
Outputs:
- ready_down: bfloat16 [256, 1024, 2048], P(('unit', 'bank'), 'zero'), parts along dimension 0
- scale_down: float32 [256, 1024], P(('unit', 'bank'), 'zero'), parts along dimension 0
- serve_router: bfloat16 [8192, 64], P('unit'), parts along dimension 0
There are 4 independent parts, one for each index of `unit`. A program takes and returns all parts, laid end to end along the dimension named above; each array names one. Nothing has to cross between parts.
All inputs are finite; a program needn't handle non-finite values.
Results may differ from a plain program's by a relative error of at most 0.001.
Values may be sent and summed in bfloat16 or wider, within the bound.
A program may use at most 256 MiB of HBM per device.

v0:
```python
import jax
import jax.numpy as jnp
from jax import lax
from jax.sharding import PartitionSpec as P


def per_device(train_down, router_weight, router_gain):
    scale_down = lax.pmax(jnp.max(jnp.abs(train_down), axis=2), "zero")
    narrow_down = (train_down / jnp.expand_dims(scale_down, 2)).astype(jnp.bfloat16)
    ready_down = lax.all_to_all(narrow_down, "zero", split_axis=1, concat_axis=2, tiled=True)
    scale_down = lax.dynamic_slice_in_dim(
        scale_down, lax.axis_index("zero") * ready_down.shape[1], ready_down.shape[1], axis=1
    )
    part_router = (router_weight * router_gain[:, None]).astype(jnp.bfloat16)
    row_router = lax.all_gather(part_router, "zero", axis=0, tiled=True)
    serve_router = lax.all_gather(row_router, "bank", axis=1, tiled=True)
    return (ready_down, scale_down, serve_router)


def solution(mesh):
    in_specs = (P(("unit", "bank"), None, "zero"), P(("unit", "zero"), "bank"), P(("unit", "zero")))
    out_specs = (P(("unit", "bank"), "zero", None), P(("unit", "bank"), "zero"), P("unit", None))
    return jax.shard_map(
        per_device, mesh=mesh, in_specs=in_specs, out_specs=out_specs, check_vma=False
    )
```

profile of v0, /device:TPU:0, one launch (start us, length us, event | category | flops | bytes accessed | tf_op | source)
XLA Modules:
  0.0 617.8 jit_solution(3817814109771987231)
XLA Ops:
  7.2 0.0 all-reduce.2.cloned.1.call-start
  7.2 21.4 %abs_reduce_fusion = f32[16,1024]{1,0:T(8,128)} fusion(f32[16,1024,1024]{2,1,0:T(8,128)} %param.3), kind=kLoop, calls=%fused_computation.2 | loop fusion | flops 33538048 | bytes 67174400 | tf_op jit(solution)/shard_map/reduce_max | solution.py:8
  28.6 0.0 all-reduce.2.cloned.1.call-update
  28.6 23.9 %all-reduce.2.cloned.1.call-done = f32[16,1024]{1,0:T(8,128)} async-done(((f32[16,1024]{1,0:T(8,128)}), f32[16,1024]{1,0:T(8,128)}) %all-reduce.2.cloned.1.call-update) | async-done | bytes 65552 | tf_op jit(solution)/shard_map/pmax | solution.py:8
  52.5 1.0 copy.7
  53.6 0.0 copy-start.1
  53.6 0.0 copy-start.2
  53.6 0.0 copy-start
  53.6 60.1 %fusion = bf16[16,1024,1024]{2,0,1:T(8,128)(2,1)} fusion(f32[16,1024,1024]{2,1,0:T(8,128)} %param.3, f32[16,1024]{0,1:T(8,128)S(1)} %copy.7), kind=kLoop, calls=%fused_computation.1 | loop fusion | flops 33554432 | bytes 100728832 | tf_op jit(solution)/shard_map/convert_element_type | solution.py:9
  113.7 13.0 %all-to-all-start = ((bf16[16,1024,1024]{2,0,1:T(8,128)(2,1)}), bf16[16,1024,1024]{2,0,1:T(8,128)(2,1)}, u32[]{:S(2)}, u32[]{:S(2)}) async-start(bf16[16,1024,1024]{2,0,1:T(8,128)(2,1)} %fusion), calls=%async_computation | async-start | bytes 67108864 | tf_op jit(solution)/shard_map/all_to_all | solution.py:10
  126.7 0.0 copy-done.1
  126.7 0.0 copy-done.2
  126.7 362.4 %all_gather.6 = bf16[2048,16]{0,1:T(8,128)(2,1)S(1)} all-gather(bf16[1024,16]{0,1:T(8,128)(2,1)S(1)} %multiply_convert_fusion), channel_id=1, replica_groups=mesh['unit'=4,'bank'=4,'zero'=2] {'zero'}, dimensions={0}, use_global_device_ids=true | all-gather | bytes 98304 | tf_op jit(solution)/shard_map/all_gather | solution.py:15
  489.1 5.8 all_gather.7
  494.9 0.0 copy-done
  494.9 0.6 constant_dynamic-slice_fusion
  495.5 0.0 all-to-all-done
  495.5 60.5 %copy.9 = bf16[16,512,2,1024]{3,2,1,0:T(2,128)(2,1)} copy(bf16[16,512,2,1024]{3,0,1,2:T(8,128)(2,1)} %bitcast.1) | data formatting | bytes 67108864 | tf_op jit(solution)/shard_map/all_to_all | solution.py:10
  556.0 54.2 %all_to_all.16 = bf16[16,512,2048]{2,1,0:T(8,128)(2,1)} reshape(bf16[16,512,2,1024]{3,2,1,0:T(2,128)(2,1)} %copy.9) | data formatting | bytes 67108864 | tf_op jit(solution)/shard_map/all_to_all | solution.py:10
  610.2 0.7 copy.15
  (1 shorter events, 0.0 us)
Async XLA Ops:
  7.2 45.4 %all-reduce.2.cloned.1.call-start = ((), (), s32[]{:S(2)}) async-start(), calls=%async_computation.1 | async-start | bytes 131072 | tf_op jit(solution)/shard_map/pmax | solution.py:8
  53.6 73.1 %copy-start.1 = (f32[1024,16]{0,1:T(8,128)S(1)}, f32[1024,16]{0,1:T(8,128)}, u32[]{:S(2)}) copy-start(f32[1024,16]{0,1:T(8,128)} %param.4) | copy-start | bytes 196612
  53.6 73.1 %copy-start.2 = (f32[1024]{0:T(1024)S(1)}, f32[1024]{0:T(1024)}, u32[]{:S(2)}) copy-start(f32[1024]{0:T(1024)} %param.5) | copy-start | bytes 12292
  53.6 441.3 %copy-start = (f32[16,1024]{1,0:T(8,128)S(1)}, f32[16,1024]{1,0:T(8,128)}, u32[]{:S(2)}) copy-start(f32[16,1024]{1,0:T(8,128)} %all-reduce.2.cloned.1.call-done) | copy-start | bytes 196612
  113.7 381.8 %all-to-all-start = ((bf16[16,1024,1024]{2,0,1:T(8,128)(2,1)}), bf16[16,1024,1024]{2,0,1:T(8,128)(2,1)}, u32[]{:S(2)}, u32[]{:S(2)}) async-start(bf16[16,1024,1024]{2,0,1:T(8,128)(2,1)} %fusion), calls=%async_computation | async-start | bytes 67108864 | tf_op jit(solution)/shard_map/all_to_all | solution.py:10
Sparse Core Ops, SparseCore 0:
  28.8 23.7 all-reduce.1
where the time goes:
time: 619 us; the launch traced here: 618 us
  blocking collectives  368 us (59%)
  local copies, waits for them, and re-layouts  117 us (19%)
  other arithmetic  81.6 us (13%)
  waiting for transfers between devices  23.9 us (4%)
  between operations  14.1 us (2%)
  starting transfers between devices  13 us (2%)
    all_gather x1, blocking collectives, per_device(): row_router = lax.all_gather(part_router, 'zero', axis=0, tiled=True)  362 us
    all_to_all x2, local copies, waits for them, and re-layouts, per_device(): lax.all_to_all(narrow_down, 'zero', split_axis=1, concat_axis=2, tiled=True)  115 us
    convert_element_type x1, other arithmetic, per_device(): (train_down / jnp.expand_dims(scale_down, 2)).astype(jnp.bfloat16)  60.1 us
    pmax x1, waiting for transfers between devices, per_device(): scale_down = lax.pmax(jnp.max(jnp.abs(train_down), axis=2), 'zero')  23.9 us
    reduce_max x1, other arithmetic, per_device(): scale_down = lax.pmax(jnp.max(jnp.abs(train_down), axis=2), 'zero')  21.4 us
    all_to_all x1, starting transfers between devices, per_device(): lax.all_to_all(narrow_down, 'zero', split_axis=1, concat_axis=2, tiled=True)  13 us
  transfers between devices with their start and end apart: 2, of which 1 were waited for; matrix products, arithmetic and copies ran while one was open for 0% of the time, Pallas kernels for 0%

commit v1 on v0

v1 whole, which is shorter than its diff:
```python
import jax
import jax.numpy as jnp
from jax import lax
from jax.experimental import pallas as pl
from jax.experimental.pallas import tpu as pltpu
from jax.sharding import PartitionSpec as P


def place_kernel(column_ref, piece_ref, *refs):
    refs[-1][...] = piece_ref[...]


def place(piece, column, first, shape, ready=None):
    experts, rows, columns = piece.shape
    in_specs = [pl.BlockSpec((1, rows, columns), lambda i, at: (i, 0, 0))]
    operands = [column, piece]
    aliases = {}
    if ready is not None:
        in_specs.append(pl.BlockSpec(memory_space=pl.ANY))
        operands.append(ready)
        aliases = {2: 0}
    return pl.pallas_call(
        place_kernel,
        out_shape=jax.ShapeDtypeStruct(shape, piece.dtype),
        grid_spec=pltpu.PrefetchScalarGridSpec(
            num_scalar_prefetch=1,
            grid=(experts,),
            in_specs=in_specs,
            out_specs=pl.BlockSpec((1, rows, columns), lambda i, at: (first + i, 0, at[0])),
        ),
        input_output_aliases=aliases,
        cost_estimate=pl.CostEstimate(
            flops=0, bytes_accessed=2 * piece.size * piece.dtype.itemsize, transcendentals=0
        ),
        name="place",
    )(*operands)


def chunks_of(experts, n):
    if n > 2 or experts < 8:
        return [experts]
    middle = experts - 5
    return [1, 1, 1] + [2] * (middle // 2) + [1] * (middle % 2) + [1, 1]


def per_device(train_down, router_weight, router_gain):
    n = lax.axis_size("zero")
    me = lax.axis_index("zero")
    experts, all_rows, columns = train_down.shape
    rows = all_rows // n
    shape = (experts, rows, n * columns)

    def shift(value, step):
        return lax.ppermute(value, "zero", [(i, (i + step) % n) for i in range(n)])

    def to_step(step):
        return lax.rem(me + step, n)

    def after(value, first):
        return lax.optimization_barrier((value, first))

    def local_max(block):
        return jnp.max(jnp.abs(block), axis=2)

    def whole_max(part):
        whole = part
        for step in range(1, n):
            whole = jnp.maximum(whole, shift(part, step))
        return whole

    def narrow(source, first, size, scale, owner):
        block = lax.dynamic_slice(source, (first, owner * rows, 0), (size, rows, columns))
        by = lax.dynamic_slice(scale, (0, owner * rows), (size, rows))
        return (block / jnp.expand_dims(by, 2)).astype(jnp.bfloat16)

    sizes = chunks_of(experts, n)
    firsts = [sum(sizes[:k]) for k in range(len(sizes))]

    groups = [(0, 1), (1, 2), (3, experts - 3)] if len(sizes) > 1 else [(0, experts)]
    scales, arrived = [], []
    source = train_down

    def find_scale(source):
        at, span = groups[len(scales)]
        part = local_max(lax.slice_in_dim(source, at, at + span, axis=0))
        source, part = after(source, part)
        scales.append(whole_max(part))
        return source

    def scale_for(first, size):
        for g, (at, span) in enumerate(groups[: len(scales)]):
            if at <= first and first + size <= at + span:
                return lax.slice_in_dim(scales[g], first - at, first - at + size, axis=0)

    for _ in range(min(2, len(groups))):
        source = find_scale(source)
    for k, (first, size) in enumerate(zip(firsts, sizes)):
        for step in range(1, n):
            piece = narrow(source, first, size, scale_for(first, size), to_step(step))
            source, piece = after(source, piece)
            arrived.append((shift(piece, step), to_step(n - step), first))
        if k == 0:
            router_weight, piece = after(router_weight, piece)
            if len(scales) < len(groups):
                source = find_scale(source)
        if k == min(5, len(sizes) - 1):
            mark = piece

    scale = jnp.concatenate([scales[g] for g in range(len(groups))], axis=0)
    own = narrow(source, 0, experts, scale, me)
    ready_down = place(own, me[None], 0, shape)
    scale_down = lax.dynamic_slice_in_dim(scale, me * rows, rows, axis=1)

    part_router = (router_weight * router_gain[:, None]).astype(jnp.bfloat16).T
    depth = part_router.shape[1]
    row_router = jnp.zeros((part_router.shape[0], n * depth), jnp.bfloat16)
    row_router = lax.dynamic_update_slice(row_router, part_router, (0, me * depth))
    for step in range(1, n):
        piece = shift(part_router, step)
        row_router = lax.dynamic_update_slice(row_router, piece, (0, to_step(n - step) * depth))
    row_router, mark = after(row_router, mark)
    serve_router = lax.all_gather(row_router, "bank", axis=0, tiled=True).T

    ready_down, _ = after(ready_down, serve_router)
    for piece, source, first in arrived:
        ready_down = place(piece, source[None], first, shape, ready_down)
    return (ready_down, scale_down, serve_router)


def solution(mesh):
    in_specs = (P(("unit", "bank"), None, "zero"), P(("unit", "zero"), "bank"), P(("unit", "zero")))
    out_specs = (P(("unit", "bank"), "zero", None), P(("unit", "bank"), "zero"), P("unit", None))
    return jax.shard_map(
        per_device, mesh=mesh, in_specs=in_specs, out_specs=out_specs, check_vma=False
    )
```

time: 619 us -> 392 us (0.63)
  blocking collectives: 368 us -> 6.23 us
  waiting for transfers between devices: 23.9 us -> 246 us
  local copies, waits for them, and re-layouts: 117 us -> 0.85 us
  Pallas kernels: 0 us -> 44.1 us
  between operations: 14.1 us -> 0.89 us
  other arithmetic: 81.6 us -> 74.6 us
    all_gather x2 -> x1, blocking collectives: 368 us -> 6.23 us  [per_device(): serve_router = lax.all_gather(row_router, 'bank', axis=0, tiled=True).T]
    ppermute x0 -> x15, waiting for transfers between devices: none -> 246 us  [shift(): return lax.ppermute(value, 'zero', [(i, (i + step) % n) for i in range(n)])]
    all_to_all x2 -> x0, local copies, waits for them, and re-layouts: 115 us -> none  [per_device(): lax.all_to_all(narrow_down, 'zero', split_axis=1, concat_axis=2, tiled=True)]
    pallas_call x0 -> x12, Pallas kernels: none -> 44.1 us  [place(): pl.pallas_call(place_kernel, out_shape=jax.ShapeDtypeStruct(shape, piece....]
    pmax x1 -> x0, waiting for transfers between devices: 23.9 us -> none  [per_device(): scale_down = lax.pmax(jnp.max(jnp.abs(train_down), axis=2), 'zero')]
    ppermute x0 -> x15, starting transfers between devices: none -> 17.4 us  [shift(): return lax.ppermute(value, 'zero', [(i, (i + step) % n) for i in range(n)])]
    all_to_all x1 -> x0, starting transfers between devices: 13 us -> none  [per_device(): lax.all_to_all(narrow_down, 'zero', split_axis=1, concat_axis=2, tiled=True)]
    convert_element_type x2 -> x12, other arithmetic: 60.1 us -> 50.7 us  [narrow(): return (block / jnp.expand_dims(by, 2)).astype(jnp.bfloat16)]
  transfers between devices with their start and end apart: 2 -> 15, of which waited for: 1 -> 4; matrix products, arithmetic and copies ran while one was open for 0% -> 19% of each run, Pallas kernels for 0% -> 11%
where the time goes in v1:
time: 392 us; the launch traced here: 390 us
  waiting for transfers between devices  246 us (63%)
  other arithmetic  74.6 us (19%)
  Pallas kernels  44.1 us (11%)
  starting transfers between devices  17.4 us (4%)
  blocking collectives  6.23 us (2%)
    ppermute x15, waiting for transfers between devices, shift(): return lax.ppermute(value, 'zero', [(i, (i + step) % n) for i in range(n)])  246 us
    convert_element_type x12, other arithmetic, narrow(): return (block / jnp.expand_dims(by, 2)).astype(jnp.bfloat16)  50.7 us
    pallas_call x12, Pallas kernels, place(): pl.pallas_call(place_kernel, out_shape=jax.ShapeDtypeStruct(shape, piece....  44.1 us
    reduce_max x3, other arithmetic, local_max(): return jnp.max(jnp.abs(block), axis=2)  23.8 us
    ppermute x15, starting transfers between devices, shift(): return lax.ppermute(value, 'zero', [(i, (i + step) % n) for i in range(n)])  17.4 us
  transfers between devices with their start and end apart: 15, of which 4 were waited for; matrix products, arithmetic and copies ran while one was open for 19% of the time, Pallas kernels for 11%

profile of v1, /device:TPU:0, one launch (start us, length us, event | category | flops | bytes accessed | tf_op | source)
XLA Modules:
  0.0 390.2 jit_solution(6497525062812419213)
XLA Ops:
  0.6 2.6 abs_reduce_fusion.2
  3.2 3.1 collective-permute-start
  6.3 4.1 %abs_reduce_fusion.1 = f32[2,1024]{1,0:T(2,128)S(1)} fusion(f32[16,1024,1024]{2,1,0:T(8,128)} %param.3), kind=kLoop, calls=%fused_computation.2 | loop fusion | flops 4192256 | bytes 8396800 | tf_op jit(solution)/shard_map/reduce_max | solution.py:63
  10.5 2.9 divide_convert_fusion.11
  15.5 17.2 %abs_reduce_fusion = f32[13,1024]{1,0:T(8,128)S(1)} fusion(f32[16,1024,1024]{2,1,0:T(8,128)} %param.3), kind=kLoop, calls=%fused_computation | loop fusion | flops 27249664 | bytes 54579200 | tf_op jit(solution)/shard_map/reduce_max | solution.py:63
  32.7 2.0 collective-permute-start.2
  36.8 3.5 collective-permute-done.14
  43.7 2.8 divide_convert_fusion.5
  46.4 2.7 divide_convert_fusion.4
  49.2 2.7 divide_convert_fusion.3
  51.9 2.0 collective-permute-start.8
  56.0 4.0 %divide_convert_fusion.2 = bf16[2,512,1024]{2,1,0:T(8,128)(2,1)} fusion(f32[16,1024,1024]{2,1,0:T(8,128)} %param.3, s32[]{:T(128)S(6)} %select_n.8, f32[2,512]{1,0:T(2,128)S(1)} %get-tuple-element.82), kind=kLoop, calls=%fused_computation.4 | loop fusion | flops 2097152 | bytes 6295556 | tf_op jit(solution)/shard_map/convert_element_type | solution.py:74
  60.0 4.0 %divide_convert_fusion.1 = bf16[2,512,1024]{2,1,0:T(8,128)(2,1)} fusion(f32[16,1024,1024]{2,1,0:T(8,128)} %param.3, s32[]{:T(128)S(6)} %select_n.8, f32[2,512]{1,0:T(2,128)S(1)} %get-tuple-element.81), kind=kLoop, calls=%fused_computation.3 | loop fusion | flops 2097152 | bytes 6295556 | tf_op jit(solution)/shard_map/convert_element_type | solution.py:74
  64.1 3.2 divide_convert_fusion.8
  67.3 2.9 divide_convert_fusion.7
  70.2 2.9 divide_convert_fusion.6
  74.9 146.6 %collective-permute-done.11.piece_ref = bf16[1,512,1024]{2,1,0:T(8,128)(2,1)S(1)} collective-permute-done((bf16[1,512,1024]{2,1,0:T(8,128)(2,1)S(1)}, bf16[1,512,1024]{2,1,0:T(8,128)(2,1)S(1)}, u32[]{:S(2)}, u32[]{:S(2)}) %collective-permute-start.11) | collective-permute-done | bytes 1048608 | tf_op jit(solution)/shard_map/ppermute | solution.py:54
  225.6 18.9 %divide_convert_fusion.piece_ref = bf16[16,512,1024]{2,1,0:T(8,128)(2,1)} fusion(f32[16,1024,1024]{2,1,0:T(8,128)} %param.3, s32[]{:T(128)S(6)} %select_n.9, f32[16,512]{1,0:T(8,128)S(1)} %fusion.2), kind=kLoop, calls=%fused_computation.1 | loop fusion | flops 16777216 | bytes 50364420 | tf_op jit(solution)/shard_map/convert_element_type | solution.py:74
  244.6 6.2 %all_gather.3 = bf16[64,2048]{1,0:T(8,128)(2,1)} all-gather(bf16[16,2048]{1,0:T(8,128)(2,1)S(1)} %constant_dynamic-update-slice_fusion), channel_id=1, replica_groups=mesh['unit'=4,'bank'=4,'zero'=2] {'bank'}, dimensions={0}, use_global_device_ids=true | all-gather | bytes 327680 | tf_op jit(solution)/shard_map/all_gather | solution.py:122
  250.8 17.4 %place.12.refs_0_ = bf16[16,512,2048]{2,1,0:T(8,128)(2,1)} custom-call(s32[1]{0:T(128)} %bitcast.8.column_ref, bf16[16,512,1024]{2,1,0:T(8,128)(2,1)} %divide_convert_fusion.piece_ref), custom_call_target="tpu_custom_call" | custom-call | bytes 33554432 | tf_op jit(solution)/shard_map/place/pallas_call | solution.py:22
  268.2 2.3 place.13.refs_0_
  270.5 2.3 place.14.refs_0_
  272.7 2.3 place.15.refs_0_
  275.0 2.6 place.16.refs_0_
  277.6 2.6 place.17.refs_0_
  280.2 2.6 place.18.refs_0_
  282.8 94.6 %collective-permute-done.7.piece_ref = bf16[2,512,1024]{2,1,0:T(8,128)(2,1)} collective-permute-done((bf16[2,512,1024]{2,1,0:T(8,128)(2,1)}, bf16[2,512,1024]{2,1,0:T(8,128)(2,1)}, u32[]{:S(2)}, u32[]{:S(2)}) %collective-permute-start.7) | collective-permute-done | bytes 2097184 | tf_op jit(solution)/shard_map/ppermute | solution.py:54
  377.4 2.6 place.19.refs_0_
  380.0 2.6 place.20.refs_0_
  382.7 2.3 place.21.refs_0_
  384.9 2.3 place.22.refs_0_
  387.2 2.3 place.23
  (64 shorter events, 16.4 us)
Async XLA Ops:
  3.2 12.1 %copy-start.8 = (f32[1024,16]{0,1:T(8,128)S(1)}, f32[1024,16]{0,1:T(8,128)}, u32[]{:S(2)}) copy-start(f32[1024,16]{0,1:T(8,128)} %param.4) | copy-start | bytes 196612
  3.2 12.1 %copy-start.9 = (f32[1024]{0:T(1024)S(1)}, f32[1024]{0:T(1024)}, u32[]{:S(2)}) copy-start(f32[1024]{0:T(1024)} %param.5) | copy-start | bytes 12292
  3.2 7.2 %collective-permute-start = (f32[1,1024]{1,0:T(1,128)S(1)}, f32[1,1024]{1,0:T(1,128)S(1)}, u32[]{:S(2)}, u32[]{:S(2)}) collective-permute-start(f32[1,1024]{1,0:T(1,128)S(1)} %bitcast.14), channel_id=1, source_target_pairs={{0,1},{1,0},{2,3},{3,2},{4,5},{5,4},{6,7},{7,6},{8,9},{9,8},{10,11... | collective-permute-start | bytes 12296 | tf_op jit(solution)/shard_map/ppermute | solution.py:54
  10.3 24.4 %collective-permute-start.1 = (f32[2,1024]{1,0:T(2,128)S(1)}, f32[2,1024]{1,0:T(2,128)S(1)}, u32[]{:S(2)}, u32[]{:S(2)}) collective-permute-start(f32[2,1024]{1,0:T(2,128)S(1)} %abs_reduce_fusion.1), channel_id=1, source_target_pairs={{0,1},{1,0},{2,3},{3,2},{4,5},{5,4},{6,7},{7,6},{8,9},{9,8},{10,11... | collective-permute-start | bytes 24584 | tf_op jit(solution)/shard_map/ppermute | solution.py:54
  13.3 50.7 %collective-permute-start.13 = (bf16[1,512,1024]{2,1,0:T(8,128)(2,1)}, bf16[1,512,1024]{2,1,0:T(8,128)(2,1)S(1)}, u32[]{:S(2)}, u32[]{:S(2)}) collective-permute-start(bf16[1,512,1024]{2,1,0:T(8,128)(2,1)} %divide_convert_fusion.11), channel_id=1, source_target_pairs={{0,1},{1,0},{2,3},{3,2},{4,5},{5,4},{6,7},{7,6},{8,9},{9,8},{10,11... | collective-permute-start | bytes 3145736 | tf_op jit(solution)/shard_map/ppermute | solution.py:54
  15.4 24.9 %collective-permute-start.14 = (bf16[16,1024]{1,0:T(8,128)(2,1)S(1)}, bf16[16,1024]{1,0:T(8,128)(2,1)S(1)}, u32[]{:S(2)}, u32[]{:S(2)}) collective-permute-start(bf16[16,1024]{1,0:T(8,128)(2,1)S(1)} %get-tuple-element.66), channel_id=1, source_target_pairs={{0,1},{1,0},{2,3},{3,2},{4,5},{5,4},{6,7},{7,6},{8,9},{9,8},{10,11... | collective-permute-start | bytes 98312 | tf_op jit(solution)/shard_map/ppermute | solution.py:54
  32.7 9.0 %collective-permute-start.2 = (f32[13,1024]{1,0:T(8,128)S(1)}, f32[13,1024]{1,0:T(8,128)S(1)}, u32[]{:S(2)}, u32[]{:S(2)}) collective-permute-start(f32[13,1024]{1,0:T(8,128)S(1)} %abs_reduce_fusion), channel_id=1, source_target_pairs={{0,1},{1,0},{2,3},{3,2},{4,5},{5,4},{6,7},{7,6},{8,9},{9,8},{10,11... | collective-permute-start | bytes 159752 | tf_op jit(solution)/shard_map/ppermute | solution.py:54
  36.7 36.5 %collective-permute-start.12 = (bf16[1,512,1024]{2,1,0:T(8,128)(2,1)S(1)}, bf16[1,512,1024]{2,1,0:T(8,128)(2,1)S(1)}, u32[]{:S(2)}, u32[]{:S(2)}) collective-permute-start(bf16[1,512,1024]{2,1,0:T(8,128)(2,1)S(1)} %divide_convert_fusion.10), channel_id=1, source_target_pairs={{0,1},{1,0},{2,3},{3,2},{4,5},{5,4},{6,7},{7,6},{8,9},{9,8},{10,11... | collective-permute-start | bytes 3145736 | tf_op jit(solution)/shard_map/ppermute | solution.py:54
  51.9 171.5 %collective-permute-start.8 = (bf16[2,512,1024]{2,1,0:T(8,128)(2,1)S(1)}, bf16[2,512,1024]{2,1,0:T(8,128)(2,1)S(1)}, u32[]{:S(2)}, u32[]{:S(2)}) collective-permute-start(bf16[2,512,1024]{2,1,0:T(8,128)(2,1)S(1)} %divide_convert_fusion.3), channel_id=1, source_target_pairs={{0,1},{1,0},{2,3},{3,2},{4,5},{5,4},{6,7},{7,6},{8,9},{9,8},{10,11... | collective-permute-start | bytes 6291464 | tf_op jit(solution)/shard_map/ppermute | solution.py:54
  53.9 169.6 %collective-permute-start.9 = (bf16[2,512,1024]{2,1,0:T(8,128)(2,1)S(1)}, bf16[2,512,1024]{2,1,0:T(8,128)(2,1)S(1)}, u32[]{:S(2)}, u32[]{:S(2)}) collective-permute-start(bf16[2,512,1024]{2,1,0:T(8,128)(2,1)S(1)} %divide_convert_fusion.4), channel_id=1, source_target_pairs={{0,1},{1,0},{2,3},{3,2},{4,5},{5,4},{6,7},{7,6},{8,9},{9,8},{10,11... | collective-permute-start | bytes 6291464 | tf_op jit(solution)/shard_map/ppermute | solution.py:54
  54.0 171.5 %collective-permute-start.10 = (bf16[2,512,1024]{2,1,0:T(8,128)(2,1)S(1)}, bf16[2,512,1024]{2,1,0:T(8,128)(2,1)S(1)}, u32[]{:S(2)}, u32[]{:S(2)}) collective-permute-start(bf16[2,512,1024]{2,1,0:T(8,128)(2,1)S(1)} %divide_convert_fusion.5), channel_id=1, source_target_pairs={{0,1},{1,0},{2,3},{3,2},{4,5},{5,4},{6,7},{7,6},{8,9},{9,8},{10,11... | collective-permute-start | bytes 6291464 | tf_op jit(solution)/shard_map/ppermute | solution.py:54
  64.0 9.0 %copy-start.3 = (bf16[1,512,1024]{2,1,0:T(8,128)(2,1)}, bf16[1,512,1024]{2,1,0:T(8,128)(2,1)S(1)}, u32[]{:S(2)}) copy-start(bf16[1,512,1024]{2,1,0:T(8,128)(2,1)S(1)} %collective-permute-done.13.piece_ref) | copy-start | bytes 3145732
  64.0 157.4 %collective-permute-start.11 = (bf16[1,512,1024]{2,1,0:T(8,128)(2,1)S(1)}, bf16[1,512,1024]{2,1,0:T(8,128)(2,1)S(1)}, u32[]{:S(2)}, u32[]{:S(2)}) collective-permute-start(bf16[1,512,1024]{2,1,0:T(8,128)(2,1)S(1)} %divide_convert_fusion.9), channel_id=1, source_target_pairs={{0,1},{1,0},{2,3},{3,2},{4,5},{5,4},{6,7},{7,6},{8,9},{9,8},{10,11... | collective-permute-start | bytes 3145736 | tf_op jit(solution)/shard_map/ppermute | solution.py:54
  73.1 171.4 %copy-start.7 = (f32[16,512]{1,0:T(8,128)}, f32[16,512]{1,0:T(8,128)S(1)}, u32[]{:S(2)}) copy-start(f32[16,512]{1,0:T(8,128)S(1)} %fusion.2) | copy-start | bytes 98308
  73.1 171.4 %copy-start.4 = (bf16[1,512,1024]{2,1,0:T(8,128)(2,1)}, bf16[1,512,1024]{2,1,0:T(8,128)(2,1)S(1)}, u32[]{:S(2)}) copy-start(bf16[1,512,1024]{2,1,0:T(8,128)(2,1)S(1)} %collective-permute-done.12.piece_ref) | copy-start | bytes 3145732
  73.2 314.0 %collective-permute-start.3 = (bf16[1,512,1024]{2,1,0:T(8,128)(2,1)}, bf16[1,512,1024]{2,1,0:T(8,128)(2,1)}, u32[]{:S(2)}, u32[]{:S(2)}) collective-permute-start(bf16[1,512,1024]{2,1,0:T(8,128)(2,1)} %divide_convert_fusion.6), channel_id=1, source_target_pairs={{0,1},{1,0},{2,3},{3,2},{4,5},{5,4},{6,7},{7,6},{8,9},{9,8},{10,11... | collective-permute-start | bytes 3145736 | tf_op jit(solution)/shard_map/ppermute | solution.py:54
  221.4 4.0 %copy-start.5 = (bf16[1,512,1024]{2,1,0:T(8,128)(2,1)}, bf16[1,512,1024]{2,1,0:T(8,128)(2,1)S(1)}, u32[]{:S(2)}) copy-start(bf16[1,512,1024]{2,1,0:T(8,128)(2,1)S(1)} %collective-permute-done.11.piece_ref) | copy-start | bytes 3145732
  221.4 163.5 %collective-permute-start.4 = (bf16[1,512,1024]{2,1,0:T(8,128)(2,1)}, bf16[1,512,1024]{2,1,0:T(8,128)(2,1)}, u32[]{:S(2)}, u32[]{:S(2)}) collective-permute-start(bf16[1,512,1024]{2,1,0:T(8,128)(2,1)} %divide_convert_fusion.7), channel_id=1, source_target_pairs={{0,1},{1,0},{2,3},{3,2},{4,5},{5,4},{6,7},{7,6},{8,9},{9,8},{10,11... | collective-permute-start | bytes 3145736 | tf_op jit(solution)/shard_map/ppermute | solution.py:54
  223.4 21.1 %copy-start = (bf16[2,512,1024]{2,1,0:T(8,128)(2,1)}, bf16[2,512,1024]{2,1,0:T(8,128)(2,1)S(1)}, u32[]{:S(2)}) copy-start(bf16[2,512,1024]{2,1,0:T(8,128)(2,1)S(1)} %collective-permute-done.8.piece_ref) | copy-start | bytes 6291460
  223.4 159.2 %collective-permute-start.5 = (bf16[1,512,1024]{2,1,0:T(8,128)(2,1)}, bf16[1,512,1024]{2,1,0:T(8,128)(2,1)}, u32[]{:S(2)}, u32[]{:S(2)}) collective-permute-start(bf16[1,512,1024]{2,1,0:T(8,128)(2,1)} %divide_convert_fusion.8), channel_id=1, source_target_pairs={{0,1},{1,0},{2,3},{3,2},{4,5},{5,4},{6,7},{7,6},{8,9},{9,8},{10,11... | collective-permute-start | bytes 3145736 | tf_op jit(solution)/shard_map/ppermute | solution.py:54
  223.5 21.0 %copy-start.1 = (bf16[2,512,1024]{2,1,0:T(8,128)(2,1)}, bf16[2,512,1024]{2,1,0:T(8,128)(2,1)S(1)}, u32[]{:S(2)}) copy-start(bf16[2,512,1024]{2,1,0:T(8,128)(2,1)S(1)} %collective-permute-done.9.piece_ref) | copy-start | bytes 6291460
  223.5 156.5 %collective-permute-start.6 = (bf16[2,512,1024]{2,1,0:T(8,128)(2,1)}, bf16[2,512,1024]{2,1,0:T(8,128)(2,1)}, u32[]{:S(2)}, u32[]{:S(2)}) collective-permute-start(bf16[2,512,1024]{2,1,0:T(8,128)(2,1)} %divide_convert_fusion.1), channel_id=1, source_target_pairs={{0,1},{1,0},{2,3},{3,2},{4,5},{5,4},{6,7},{7,6},{8,9},{9,8},{10,11... | collective-permute-start | bytes 6291464 | tf_op jit(solution)/shard_map/ppermute | solution.py:54
  225.5 19.1 %copy-start.2 = (bf16[2,512,1024]{2,1,0:T(8,128)(2,1)}, bf16[2,512,1024]{2,1,0:T(8,128)(2,1)S(1)}, u32[]{:S(2)}) copy-start(bf16[2,512,1024]{2,1,0:T(8,128)(2,1)S(1)} %collective-permute-done.10.piece_ref) | copy-start | bytes 6291460
  225.5 152.0 %collective-permute-start.7 = (bf16[2,512,1024]{2,1,0:T(8,128)(2,1)}, bf16[2,512,1024]{2,1,0:T(8,128)(2,1)}, u32[]{:S(2)}, u32[]{:S(2)}) collective-permute-start(bf16[2,512,1024]{2,1,0:T(8,128)(2,1)} %divide_convert_fusion.2), channel_id=1, source_target_pairs={{0,1},{1,0},{2,3},{3,2},{4,5},{5,4},{6,7},{7,6},{8,9},{9,8},{10,11... | collective-permute-start | bytes 6291464 | tf_op jit(solution)/shard_map/ppermute | solution.py:54
  387.2 2.3 copy-start.6
